TPU v7x, 32 devices: a whole 2x2x4 slice. The times are simulated.
32 devices in a mesh: grp: 4 (over x, core), pages: 8 (over z, y).
Axes of the slice: x: 2, y: 2, z: 4, core: 2. Of those that a mesh axis runs over, the one named last changes fastest.
Arguments:
- queries: bfloat16 [128, 64, 2048], P(('grp', 'pages')), parts along dimension 0, may hold values from -500 to 500
- tree_keys: bfloat16 [128, 64, 512], P(('grp', 'pages')), parts along dimension 0, may hold values from -6 to 6
- tree_values: bfloat16 [128, 64, 512], P(('grp', 'pages')), parts along dimension 0, may hold values from -6 to 6
- page_keys: bfloat16 [256, 256, 512], P(('grp', 'pages')), parts along dimension 0, may hold values from -6 to 6
- page_values: bfloat16 [256, 256, 512], P(('grp', 'pages')), parts along dimension 0, may hold values from -6 to 6
- page_table: int32 [128, 4], P(('grp', 'pages')), parts along dimension 0, may hold values from 0 to 63, as said below
- prefix_lengths: int32 [128], P(('grp', 'pages')), parts along dimension 0, may hold values from 513 to 1024
- tree_parents: int32 [128, 64], P(('grp', 'pages')), parts along dimension 0, may hold values from -1 to 62, as said below
- live_lengths: int32 [128], P(('grp', 'pages')), parts along dimension 0, may hold values from 1 to 64
Outputs:
- attended: bfloat16 [128, 64, 2048], P(('grp', 'pages')), parts along dimension 0
- page_reads: int32 [256], P(('grp', 'pages')), parts along dimension 0
There are 4 independent parts, one for each index of `grp`. A program takes and returns all parts, laid end to end along the dimension named above; each array names one. Nothing has to cross between parts.
Inputs may be any that keep to these rules, and one draw needn't show every extreme that they name: `page_table`: the owner of page p is index p // 8 along pages. Over the rows of one device, the used slots name pages of any one owner at most 2 times, and in every draw each device names some owner exactly 2 times. `tree_parents`: entry t is -1 for t = 0 and a number below t otherwise.
All inputs are finite; a program needn't handle non-finite values.
Results may differ from a plain program's by a relative error of at most 0.0085.
Values may be sent and summed in bfloat16 or wider, within the bound.
A program may use at most 192 MiB of HBM per device.

v0:
```python
import jax
import jax.numpy as jnp
from jax import lax
from jax.sharding import PartitionSpec as P

QH = 16
KVH = 4
HD = 128


NEG_BIG = -1e30


def ancestry(parents):
    tree_size = parents.shape[1]
    index = jnp.arange(tree_size, dtype=jnp.int32)
    links = (index[None, None, :] == parents[:, :, None]) | (
        index[None, :, None] == index[None, None, :]
    )
    reach = links.astype(jnp.float32)
    for level in range((tree_size - 1).bit_length()):
        reach = (
            jnp.einsum("rts,rsu->rtu", reach, reach, precision=lax.Precision.HIGHEST) > 0
        ).astype(jnp.float32)
    return reach


def tree_parts(queries, keys, values, reach, live):
    groups = QH // KVH
    count, tree_size = (queries.shape[0], queries.shape[1])
    query = queries.reshape(count, tree_size, KVH, groups, HD)
    keyed = keys.reshape(count, tree_size, KVH, HD)
    valued = values.reshape(count, tree_size, KVH, HD)
    score_values = jnp.einsum(
        "rtkgd,rskd->rkgts", query, keyed, preferred_element_type=jnp.float32
    ) * HD ** (-0.5)
    allowed = (reach > 0) & (
        jnp.arange(tree_size, dtype=jnp.int32)[None, None, :] < live[:, None, None]
    )
    score_values = jnp.where(allowed[:, None, None, :, :], score_values, NEG_BIG)
    peak = jnp.max(score_values, axis=-1)
    expo = jnp.exp(score_values - peak[..., None])
    total = jnp.sum(expo, axis=-1)
    weights = expo.astype(jnp.bfloat16)
    out = jnp.einsum("rkgts,rskd->rtkgd", weights, valued, preferred_element_type=jnp.float32)
    out = out.reshape(count, tree_size, QH, HD)
    peak = peak.transpose(0, 3, 1, 2).reshape(count, tree_size, QH)
    total = total.transpose(0, 3, 1, 2).reshape(count, tree_size, QH)
    return (peak, total, out)


def page_parts(asked, keys, values, counts):
    groups = QH // KVH
    items, tree_size = (asked.shape[0], asked.shape[1])
    query = asked.reshape(items, tree_size, KVH, groups, HD)
    keyed = keys.reshape(items, -1, KVH, HD)
    valued = values.reshape(items, -1, KVH, HD)
    score_values = jnp.einsum(
        "btkgd,bpkd->bkgtp", query, keyed, preferred_element_type=jnp.float32
    ) * HD ** (-0.5)
    allowed = jnp.arange(keyed.shape[1], dtype=jnp.int32)[None, :] < counts[:, None]
    score_values = jnp.where(allowed[:, None, None, None, :], score_values, NEG_BIG)
    peak = jnp.max(score_values, axis=-1)
    expo = jnp.exp(score_values - peak[..., None])
    total = jnp.sum(expo, axis=-1)
    weights = expo.astype(jnp.bfloat16)
    out = jnp.einsum("bkgtp,bpkd->btkgd", weights, valued, preferred_element_type=jnp.float32)
    out = out.astype(jnp.bfloat16).reshape(items, tree_size, QH * HD)
    peak = peak.transpose(0, 3, 1, 2).reshape(items, tree_size, QH)
    total = total.transpose(0, 3, 1, 2).reshape(items, tree_size, QH)
    return (peak, total, out)


def shards(
    queries,
    tree_keys,
    tree_values,
    page_keys,
    page_values,
    page_table,
    prefix_lengths,
    tree_parents,
    live_lengths,
):
    devices = lax.axis_size("pages")
    req_count, tree_size, width = queries.shape
    pages_here, page_size = (page_keys.shape[0], page_keys.shape[1])
    slot_count = page_table.shape[1]
    capacity = max(1, req_count * slot_count // devices)
    pair_count = req_count * slot_count
    request_index = jnp.tile(jnp.arange(req_count, dtype=jnp.int32), slot_count)
    slot_index = jnp.repeat(jnp.arange(slot_count, dtype=jnp.int32), req_count)
    page_ids = page_table.T.reshape(-1)
    key_counts = jnp.clip(prefix_lengths[request_index] - slot_index * page_size, 0, page_size)
    used = key_counts > 0
    owners = page_ids // pages_here
    local_pages = page_ids % pages_here
    pair_index = jnp.arange(pair_count, dtype=jnp.int32)
    earlier = (
        (owners[:, None] == owners[None, :])
        & used[None, :]
        & (pair_index[None, :] < pair_index[:, None])
    )
    ranks = jnp.sum(earlier.astype(jnp.int32), axis=1)
    targets = jnp.where(used, owners * capacity + ranks, -1)
    placed = jnp.arange(devices * capacity, dtype=jnp.int32)[:, None] == targets[None, :]
    slot_page = jnp.sum(jnp.where(placed, local_pages[None, :], 0), axis=1)
    slot_keys = jnp.sum(jnp.where(placed, key_counts[None, :], 0), axis=1)
    labels_out = jnp.stack([slot_page, slot_keys], axis=-1).reshape(devices, capacity, 2)
    fetch = jnp.maximum(targets, 0)
    wanted = lax.all_to_all(labels_out, "pages", split_axis=0, concat_axis=0, tiled=True)[..., 0]
    key_slots = lax.all_to_all(page_keys[wanted], "pages", split_axis=0, concat_axis=0, tiled=True)
    value_slots = lax.all_to_all(
        page_values[wanted], "pages", split_axis=0, concat_axis=0, tiled=True
    )
    fetched_keys = key_slots.reshape(devices * capacity, page_size, -1)[fetch]
    fetched_values = value_slots.reshape(devices * capacity, page_size, -1)[fetch]
    page_maximum, page_total, page_out = page_parts(
        queries[request_index], fetched_keys, fetched_values, key_counts
    )
    page_maximum = page_maximum.reshape(slot_count, req_count, tree_size, QH)
    page_total = page_total.reshape(slot_count, req_count, tree_size, QH)
    page_out = page_out.reshape(slot_count, req_count, tree_size, QH, HD)
    usable = used.reshape(slot_count, req_count)[:, :, None, None]
    reach = ancestry(tree_parents)
    tree_peak, tree_total, tree_out = tree_parts(
        queries, tree_keys, tree_values, reach, live_lengths
    )
    masked = jnp.where(usable, page_maximum, NEG_BIG)
    top = jnp.maximum(tree_peak, jnp.max(masked, axis=0))
    tree_scale = jnp.exp(tree_peak - top)
    page_scale = jnp.where(usable, jnp.exp(masked - top[None]), 0.0)
    total = tree_total * tree_scale + jnp.sum(page_scale * page_total, axis=0)
    mixed = tree_out * tree_scale[..., None] + jnp.sum(
        page_scale[..., None] * page_out.astype(jnp.float32), axis=0
    )
    attended = (mixed / total[..., None]).reshape(req_count, tree_size, width).astype(jnp.bfloat16)
    all_pages = jnp.arange(devices * pages_here, dtype=jnp.int32)
    weight = jnp.where(used, live_lengths[request_index], 0).astype(jnp.float32)
    term = jnp.sum(jnp.where(page_ids[:, None] == all_pages[None, :], weight[:, None], 0.0), axis=0)
    reads = lax.psum_scatter(term, "pages", scatter_dimension=0, tiled=True)
    return (attended, reads.astype(jnp.int32))


def solution(mesh):
    return jax.shard_map(
        shards,
        mesh=mesh,
        in_specs=(
            P(("grp", "pages"), None, None),
            P(("grp", "pages"), None, None),
            P(("grp", "pages"), None, None),
            P(("grp", "pages"), None, None),
            P(("grp", "pages"), None, None),
            P(("grp", "pages"), None),
            P(("grp", "pages")),
            P(("grp", "pages"), None),
            P(("grp", "pages")),
        ),
        out_specs=(P(("grp", "pages"), None, None), P(("grp", "pages"))),
        check_vma=False,
    )
```

profile of v0, /device:TPU:8, one launch (start us, length us, event | category | flops | bytes accessed | tf_op | source)
XLA Modules:
  0.0 291.4 jit_solution(17695682487890688429)
XLA Ops:
  0.6 0.0 copy-start
  0.7 0.1 tile.18
  0.8 1.4 gather_fusion
  2.2 1.3 gather_fusion.6
  3.5 0.1 mul.105
  3.6 0.8 copy.92
  4.4 0.1 reshape.411
  4.5 0.2 convert_reduce_fusion
  4.7 0.1 select_reduce_fusion.3
  4.8 0.1 stack.10
  4.9 0.1 stack.9
  5.0 11.1 %all_to_all.15 = s32[8,2,2]{1,2,0:T(2,128)S(1)} all-to-all(s32[8,2,2]{1,2,0:T(2,128)S(1)} %copy.93), channel_id=1, replica_groups=mesh['grp'=4,'pages'=8] {'pages'}, dimensions={0} | all-to-all | bytes 256 | tf_op jit(solution)/shard_map/all_to_all | solution.py:111
  16.1 0.1 reshape.430
  16.2 2.7 gather_fusion.1
  19.0 6.1 %all-to-all-start.1 = ((bf16[8,2,256,512]{3,2,1,0:T(8,128)(2,1)}), bf16[8,2,256,512]{3,2,1,0:T(8,128)(2,1)}, u32[]{:S(2)}, u32[]{:S(2)}) async-start(bf16[8,2,256,512]{3,2,1,0:T(8,128)(2,1)} %bitcast.94), calls=%async_computation.1 | async-start | bytes 8388608 | tf_op jit(solution)/shard_map/all_to_all | solution.py:112
  25.1 2.8 gather_fusion.4
  27.9 86.8 %all-to-all-done.1 = bf16[8,2,256,512]{3,2,1,0:T(8,128)(2,1)} async-done(((bf16[8,2,256,512]{3,2,1,0:T(8,128)(2,1)}), bf16[8,2,256,512]{3,2,1,0:T(8,128)(2,1)}, u32[]{:S(2)}, u32[]{:S(2)}) %all-to-all-start.1) | async-done | bytes 4194336 | tf_op jit(solution)/shard_map/all_to_all | solution.py:112
  114.7 7.1 %all-to-all-start.2 = ((bf16[8,2,256,512]{3,2,1,0:T(8,128)(2,1)}), bf16[8,2,256,512]{3,2,1,0:T(8,128)(2,1)}, u32[]{:S(2)}, u32[]{:S(2)}) async-start(bf16[8,2,256,512]{3,2,1,0:T(8,128)(2,1)} %bitcast.93), calls=%async_computation.2 | async-start | bytes 8388608 | tf_op jit(solution)/shard_map/all_to_all | solution.py:113
  121.8 0.1 mul.107
  121.9 0.1 reshape.413
  122.0 0.1 gather.26
  122.0 2.8 gather_fusion.3
  124.8 0.7 reshape.407
  125.6 0.0 copy-start.10
  125.6 0.0 copy-start.8
  125.6 0.0 copy-start.9
  125.6 7.8 %reshape.415 = bf16[16,64,4,4,128]{4,3,2,1,0:T(4,128)(2,1)} reshape(bf16[16,64,2048]{2,1,0:T(8,128)(2,1)} %gather_fusion.3) | data formatting | bytes 8388608 | tf_op jit(solution)/shard_map/reshape | solution.py:55
  133.4 0.3 fusion.35
  133.7 0.2 fusion.36
  133.9 0.2 fusion.37
  134.1 0.2 fusion.38
  134.3 0.2 fusion.39
  134.5 0.1 iota_compare_fusion.6
  134.6 0.2 fusion.34
  134.8 0.1 copy.86
  134.9 0.8 reshape.406
  135.7 0.1 reshape.408
  135.8 2.1 fusion.65
  137.9 0.5 convolution_bitcast_fusion
  138.5 2.7 copy.91
  141.2 3.0 %reshape.409 = f32[4,64,2048]{2,1,0:T(8,128)} reshape(f32[4,64,4,4,128]{4,3,2,1,0:T(4,128)} %copy.91) | data formatting | bytes 4194304 | tf_op jit(solution)/shard_map/reshape | solution.py:46
  144.2 0.6 dynamic-slice
  145.5 0.1 select_reduce_fusion.1
  145.5 76.7 %all-reduce = f32[64]{0:T(128)S(1)} all-reduce(f32[64]{0:T(128)S(1)} %select_reduce_fusion.1), channel_id=2, replica_groups=mesh['grp'=4,'pages'=8] {'pages'}, use_global_device_ids=true, to_apply=%region_11.12.clone | all-reduce | flops 64 | bytes 512
  222.2 0.6 dynamic-slice_convert_fusion
  222.8 0.5 fusion.15
  223.3 0.1 iota_compare_fusion.2
  223.4 5.0 %gather_fusion.2 = bf16[16,256,512]{2,1,0:T(8,128)(2,1)} fusion(bf16[16,256,512]{2,1,0:T(8,128)(2,1)} %bitcast.10, s32[1024]{0:T(1024)S(1)} %pad_clamp_fusion), kind=kCustom, calls=%fused_computation.2 | custom fusion | bytes 8388672 | tf_op jit(solution)/shard_map/gather | solution.py:116
  228.4 6.4 %copy.95 = bf16[16,256,512]{1,2,0:T(8,128)(2,1)} copy(bf16[16,256,512]{2,1,0:T(8,128)(2,1)} %gather_fusion.2) | data formatting | bytes 8388608 | tf_op jit(solution)/shard_map/gather | solution.py:116
  234.8 5.0 %gather_fusion.5 = bf16[16,256,512]{2,1,0:T(8,128)(2,1)} fusion(bf16[16,256,512]{2,1,0:T(8,128)(2,1)} %bitcast.20, s32[1024]{0:T(1024)S(1)} %pad_clamp_fusion), kind=kCustom, calls=%fused_computation.5 | custom fusion | bytes 8388672 | tf_op jit(solution)/shard_map/gather | solution.py:117
  239.8 6.4 %copy.99 = bf16[16,256,512]{1,2,0:T(8,128)(2,1)} copy(bf16[16,256,512]{2,1,0:T(8,128)(2,1)} %gather_fusion.5) | data formatting | bytes 8388608 | tf_op jit(solution)/shard_map/gather | solution.py:117
  246.1 12.2 %bitcast_reduce_fusion = (f32[16,4,4,64]{3,2,1,0:T(4,128)S(1)}, f32[16,4,256,64,4]{2,3,4,1,0:T(8,128)}) fusion(pred[16,256]{1,0:T(8,128)(4,1)S(1)} %iota_compare_fusion.2, bf16[16,256,4,128,1]{1,3,4,2,0:T(8,128)(2,1)} %bitcast.95, bf16[16,64,4,4,128]{4,3,2,1,0:T(4,128)(2,1)} %reshape.415), kind=kOutput, calls=%fused_computation.8 | convolution fusion | flops 1086308352 | bytes 25235456 | tf_op jit(solution)/shard_map/btkgd,bpkd->bkgtp/dot_general | solution.py:58
  258.3 8.9 %fusion.1 = f32[16,4,4,64]{3,2,1,0:T(4,128)S(1)} fusion(f32[16,4,256,64,4]{2,3,4,1,0:T(8,128)} %get-tuple-element.13, f32[16,4,4,64]{3,2,1,0:T(4,128)S(1)} %get-tuple-element.12, pred[16,256]{1,0:T(8,128)(4,1)S(1)} %iota_compare_fusion.2), kind=kLoop, calls=%fused_computation.11 | loop fusion | flops 16760832 | bytes 16912384 | tf_op jit(solution)/shard_map/reduce_sum | solution.py:65
  267.2 11.2 %convert_convert_fusion = f32[16,4,128,4,64]{2,4,3,1,0:T(8,128)} fusion(bf16[16,256,4,128,1]{1,3,4,2,0:T(8,128)(2,1)} %bitcast.96, f32[16,4,256,64,4]{2,3,4,1,0:T(8,128)} %get-tuple-element.13, f32[16,4,4,64]{3,2,1,0:T(4,128)S(1)} %get-tuple-element.12, pred[16,256]{1,0:T(8,128)(4,1)S(1)} %iota_compare_fusion.2), kind=kOutput, calls=%fused_computation.21 | convolution fusion | flops 1094713344 | bytes 29429760 | tf_op jit(solution)/shard_map/bkgtp,bpkd->btkgd/dot_general | solution.py:67
  278.4 0.1 select_reduce_fusion
  278.5 0.1 multiply_reduce_fusion.1
  278.7 0.1 copy.102
  278.8 0.6 div.39
  279.4 1.6 div.40
  281.0 0.1 copy.98
  281.1 0.6 mul.111
  281.7 1.5 mul.112
  283.2 6.6 %multiply_reduce_fusion = f32[4,64,16,128]{3,1,2,0:T(8,128)S(1)} fusion(f32[4,4,64,16,128]{4,2,3,1,0:T(8,128)} %bitcast.92, f32[4,4,64,16]{2,3,1,0:T(8,128)S(1)} %get-tuple-element.9), kind=kLoop, calls=%fused_computation.14 | loop fusion | flops 3670016 | bytes 10551296 | tf_op jit(solution)/shard_map/reduce_sum | solution.py:134
  289.7 1.7 fusion.14
  (44 shorter events, 0.4 us)
Async XLA Ops:
  0.6 15.6 %copy-start = (bf16[8,256,512]{2,1,0:T(8,128)(2,1)S(1)}, bf16[8,256,512]{2,1,0:T(8,128)(2,1)}, u32[]{:S(2)}) copy-start(bf16[8,256,512]{2,1,0:T(8,128)(2,1)} %param.12) | copy-start | bytes 6291460
  19.0 6.1 %copy-start.4 = (bf16[8,256,512]{2,1,0:T(8,128)(2,1)S(1)}, bf16[8,256,512]{2,1,0:T(8,128)(2,1)}, u32[]{:S(2)}) copy-start(bf16[8,256,512]{2,1,0:T(8,128)(2,1)} %param.13) | copy-start | bytes 6291460
  19.0 95.7 %all-to-all-start.1 = ((bf16[8,2,256,512]{3,2,1,0:T(8,128)(2,1)}), bf16[8,2,256,512]{3,2,1,0:T(8,128)(2,1)}, u32[]{:S(2)}, u32[]{:S(2)}) async-start(bf16[8,2,256,512]{3,2,1,0:T(8,128)(2,1)} %bitcast.94), calls=%async_computation.1 | async-start | bytes 8388608 | tf_op jit(solution)/shard_map/all_to_all | solution.py:112
  114.7 7.4 %copy-start.3 = (bf16[4,64,2048]{2,1,0:T(8,128)(2,1)S(1)}, bf16[4,64,2048]{2,1,0:T(8,128)(2,1)}, u32[]{:S(2)}) copy-start(bf16[4,64,2048]{2,1,0:T(8,128)(2,1)} %param.9) | copy-start | bytes 3145732
  114.7 120.1 %all-to-all-start.2 = ((bf16[8,2,256,512]{3,2,1,0:T(8,128)(2,1)}), bf16[8,2,256,512]{3,2,1,0:T(8,128)(2,1)}, u32[]{:S(2)}, u32[]{:S(2)}) async-start(bf16[8,2,256,512]{3,2,1,0:T(8,128)(2,1)} %bitcast.93), calls=%async_computation.2 | async-start | bytes 8388608 | tf_op jit(solution)/shard_map/all_to_all | solution.py:113
  125.6 7.8 %copy-start.10 = (s32[4,64]{1,0:T(4,128)S(1)}, s32[4,64]{1,0:T(4,128)}, u32[]{:S(2)}) copy-start(s32[4,64]{1,0:T(4,128)} %param.16) | copy-start | bytes 3076
  125.6 8.9 %copy-start.2 = (s32[4]{0:T(128)S(1)}, s32[4]{0:T(128)}, u32[]{:S(2)}) copy-start(s32[4]{0:T(128)} %param.17) | copy-start | bytes 52
  125.6 9.3 %copy-start.8 = (bf16[4,64,512]{2,1,0:T(8,128)(2,1)S(1)}, bf16[4,64,512]{2,1,0:T(8,128)(2,1)}, u32[]{:S(2)}) copy-start(bf16[4,64,512]{2,1,0:T(8,128)(2,1)} %param.10) | copy-start | bytes 786436
  125.6 10.1 %copy-start.9 = (bf16[4,64,512]{2,1,0:T(8,128)(2,1)S(1)}, bf16[4,64,512]{2,1,0:T(8,128)(2,1)}, u32[]{:S(2)}) copy-start(bf16[4,64,512]{2,1,0:T(8,128)(2,1)} %param.11) | copy-start | bytes 786436
  138.4 5.8 %copy-start.11 = (u32[32]{0:T(128)S(1)}, u32[32]{0:T(128)}, u32[]{:S(2)}) copy-start(u32[32]{0:T(128)} %constant.63) | copy-start | bytes 388
  283.1 6.6 %copy-start.5 = (f32[4,64,2048]{2,1,0:T(8,128)S(1)}, f32[4,64,2048]{2,1,0:T(8,128)}, u32[]{:S(2)}) copy-start(f32[4,64,2048]{2,1,0:T(8,128)} %reshape.409) | copy-start | bytes 6291460
  283.1 6.6 %copy-start.6 = (f32[4,64,2048]{2,1,0:T(8,128)S(1)}, f32[4,64,2048]{2,1,0:T(8,128)}, u32[]{:S(2)}) copy-start(f32[4,64,2048]{2,1,0:T(8,128)} %div.40) | copy-start | bytes 6291460
  283.1 6.6 %copy-start.7 = (f32[4,64,2048]{2,1,0:T(8,128)S(1)}, f32[4,64,2048]{2,1,0:T(8,128)}, u32[]{:S(2)}) copy-start(f32[4,64,2048]{2,1,0:T(8,128)} %mul.112) | copy-start | bytes 6291460
  283.1 8.3 %copy-start.1 = (bf16[8,256,512]{2,1,0:T(8,128)(2,1)S(1)}, bf16[8,256,512]{2,1,0:T(8,128)(2,1)}, u32[]{:S(2)}) copy-start(bf16[8,256,512]{2,1,0:T(8,128)(2,1)} %param.12) | copy-start | bytes 6291460
where the time goes:
time: 292 us; the launch traced here: 291 us
  blocking collectives  87.8 us (30%)
  waiting for transfers between devices  86.8 us (30%)
  local copies, waits for them, and re-layouts  55.6 us (19%)
  matrix products  27.2 us (9%)
  other arithmetic  19.3 us (7%)
  starting transfers between devices  13.2 us (5%)
    all_to_all x1, waiting for transfers between devices, shards(): lax.all_to_all(page_keys[wanted], 'pages', split_axis=0, concat_axis=0, t...  86.8 us
    unnamed x1, blocking collectives  76.7 us
    dot_general x1, matrix products, page_parts(): jnp.einsum('btkgd,bpkd->bkgtp', query, keyed, preferred_element_type=jnp....  12.2 us
    gather x2, local copies, waits for them, and re-layouts, shards(): fetched_keys = key_slots.reshape(devices * capacity, page_size, -1)[fetch]  11.4 us
    gather x2, local copies, waits for them, and re-layouts, shards(): value_slots.reshape(devices * capacity, page_size, -1)[fetch]  11.3 us
    dot_general x1, matrix products, page_parts(): jnp.einsum('bkgtp,bpkd->btkgd', weights, valued, preferred_element_type=j...  11.2 us
    all_to_all x1, blocking collectives, shards(): lax.all_to_all(labels_out, 'pages', split_axis=0, concat_axis=0, tiled=True)  11.1 us
    reduce_sum x1, other arithmetic, page_parts(): total = jnp.sum(expo, axis=-1)  8.87 us
  transfers between devices with their start and end apart: 2, of which 1 were waited for; matrix products, arithmetic and copies ran while one was open for 13% of the time, Pallas kernels for 0%

commit v1 on v0

v1 whole, which is shorter than its diff:
```python
import functools

import jax
import jax.numpy as jnp
from jax import lax
from jax.experimental import pallas as pl
from jax.experimental.pallas import tpu as pltpu
from jax.sharding import PartitionSpec as P

QH = 16
KVH = 4
HD = 128
GROUPS = QH // KVH
NEG_BIG = -1e30
SCALE = HD ** (-0.5)
NT = (((1,), (1,)), ((), ()))
MESH = pl.DeviceIdType.MESH


def head(h):
    return slice(h * HD, (h + 1) * HD)


def attend(query_of, keys_of, values_of, allowed, out_to, stats, lane, first):
    for k in range(KVH):
        query = jnp.concatenate([query_of(k * GROUPS + g) for g in range(GROUPS)], axis=0)
        scores = (
            lax.dot_general(query, keys_of(k), NT, preferred_element_type=jnp.float32) * SCALE
        )
        scores = jnp.where(allowed, scores, NEG_BIG)
        peak = jnp.max(scores, axis=-1, keepdims=True)
        expo = jnp.exp(scores - peak)
        total = jnp.sum(expo, axis=-1, keepdims=True)
        out = jnp.dot(
            expo.astype(jnp.bfloat16), values_of(k), preferred_element_type=jnp.float32
        )
        rows = out.shape[0] // GROUPS
        for g in range(GROUPS):
            h = k * GROUPS + g
            part = slice(g * rows, (g + 1) * rows)
            out_to(h, out[part])
            stats = jnp.where(lane == first + h, peak[part], stats)
            stats = jnp.where(lane == first + QH + h, total[part], stats)
    return stats


def exchange(
    n,
    cap,
    meta,
    live,
    q_ref,
    tk_ref,
    tv_ref,
    link_ref,
    pk_ref,
    pv_ref,
    got_out,
    got_stats,
    tree_out,
    tree_stats,
    q_all,
    q_now,
    out_send,
    stats_send,
    q_send_sem,
    q_recv_sem,
    out_send_sem,
    out_recv_sem,
    stats_send_sem,
    stats_recv_sem,
    local_sem,
):
    reqs, tree, _ = q_ref.shape
    page = pk_ref.shape[1]
    depth = n // 2
    me = lax.axis_index("pages")
    z, y = me // 2, me % 2
    other = 1 - y
    partner = z * 2 + other

    barrier = pltpu.get_barrier_semaphore()

    def greet(i, _):
        pl.semaphore_signal(
            barrier, inc=1, device_id={"pages": (me + i) % n}, device_id_type=MESH
        )
        return 0

    lax.fori_loop(1, n, greet, 0)
    pl.semaphore_wait(barrier, n - 1)

    def q_copy(src_ref, src, i, way, to):
        return pltpu.make_async_remote_copy(
            src_ref=src_ref,
            dst_ref=q_all.at[src, i],
            send_sem=q_send_sem.at[way, src // 2, i],
            recv_sem=q_recv_sem.at[src, i],
            device_id={"pages": to},
            device_id_type=MESH,
        )

    def out_copy(d):
        return pltpu.make_async_remote_copy(
            src_ref=out_send.at[d],
            dst_ref=got_out.at[me],
            send_sem=out_send_sem.at[d],
            recv_sem=out_recv_sem.at[me],
            device_id={"pages": d},
            device_id_type=MESH,
        )

    def stats_copy(d):
        return pltpu.make_async_remote_copy(
            src_ref=stats_send.at[d],
            dst_ref=got_stats.at[me],
            send_sem=stats_send_sem.at[d],
            recv_sem=stats_recv_sem.at[me],
            device_id={"pages": d},
            device_id_type=MESH,
        )

    def q_arrive(src, i):
        pltpu.make_async_remote_copy(
            src_ref=q_all.at[src, i],
            dst_ref=q_all.at[src, i],
            send_sem=q_send_sem.at[0, src // 2, i],
            recv_sem=q_recv_sem.at[src, i],
            device_id={"pages": partner},
            device_id_type=MESH,
        ).wait_recv()

    for i in range(reqs):
        q_copy(q_ref.at[i], me, i, 2, partner).start()

        @pl.when(z + 1 < depth)
        def _():
            q_copy(q_ref.at[i], me, i, 0, me + 2).start()

        @pl.when(z > 0)
        def _():
            q_copy(q_ref.at[i], me, i, 1, me - 2).start()

    lane = lax.broadcasted_iota(jnp.int32, (tree, HD), 1)
    key_lane = lax.broadcasted_iota(jnp.int32, (GROUPS * tree, page), 1)

    def serve(d):
        stats = jnp.zeros((tree, HD), jnp.float32)
        for c in range(cap):
            base = (d * cap + c) * 3
            which, count, req = meta[base], meta[base + 1], meta[base + 2]

            def out_to(h, value):
                out_send[d, c, :, head(h)] = value.astype(jnp.bfloat16)

            stats = attend(
                lambda h: q_now[req, :, head(h)],
                lambda k: pk_ref[which, :, head(k)],
                lambda k: pv_ref[which, :, head(k)],
                key_lane < count,
                out_to,
                stats,
                lane,
                c * 2 * QH,
            )
        stats_send[d] = stats

    q_now[...] = q_ref[...]
    serve(me)
    own_out = pltpu.make_async_copy(out_send.at[me], got_out.at[me], local_sem.at[0])
    own_stats = pltpu.make_async_copy(stats_send.at[me], got_stats.at[me], local_sem.at[1])
    own_out.start()
    own_stats.start()

    def one_tree(r, _):
        reach = link_ref[r]
        for level in range((tree - 1).bit_length()):
            reach = jnp.where(
                jnp.dot(reach, reach, preferred_element_type=jnp.float32) > 0, 1.0, 0.0
            ).astype(jnp.bfloat16)
        seen = lax.broadcasted_iota(jnp.int32, (tree, tree), 1) < live[r]
        open_ = jnp.where(seen, reach.astype(jnp.float32), 0.0)
        allowed = jnp.concatenate([open_] * GROUPS, axis=0) > 0

        def out_to(h, value):
            tree_out[r, :, head(h)] = value

        tree_stats[r] = attend(
            lambda h: q_ref[r, :, head(h)],
            lambda k: tk_ref[r, :, head(k)],
            lambda k: tv_ref[r, :, head(k)],
            allowed,
            out_to,
            jnp.zeros((tree, HD), jnp.float32),
            lane,
            0,
        )
        return 0

    lax.fori_loop(0, reqs, one_tree, 0)

    def step(s, _):
        for i in range(reqs):

            @pl.when(z - s >= 0)
            def _():
                src = me - 2 * s
                q_arrive(src, i)
                q_copy(q_all.at[src, i], src, i, 2, partner).start()

                @pl.when(z + 1 < depth)
                def _():
                    q_copy(q_all.at[src, i], src, i, 0, me + 2).start()

            @pl.when(z + s < depth)
            def _():
                src = me + 2 * s
                q_arrive(src, i)
                q_copy(q_all.at[src, i], src, i, 2, partner).start()

                @pl.when(z > 0)
                def _():
                    q_copy(q_all.at[src, i], src, i, 1, me - 2).start()

        def case(k, _):
            crossed = k // 2
            far = s - crossed
            row = z + far * (2 * (k % 2) - 1)
            column = y + crossed * (other - y)
            d = row * 2 + column
            valid = (row >= 0) & (row < depth) & ((far > 0) | (k == 2))

            @pl.when(valid)
            def _():
                @pl.when(crossed == 1)
                def _():
                    for i in range(reqs):
                        q_arrive(d, i)

                q_now[...] = q_all[d]
                serve(d)
                out_copy(d).start()
                stats_copy(d).start()

            return 0

        lax.fori_loop(0, 4, case, 0)
        return 0

    lax.fori_loop(1, depth + 1, step, 0)

    own_out.wait()
    own_stats.wait()

    def finish(i, _):
        d = (me + i) % n
        out_copy(d).wait_send()
        stats_copy(d).wait_send()
        pltpu.make_async_remote_copy(
            src_ref=out_send.at[d],
            dst_ref=got_out.at[d],
            send_sem=out_send_sem.at[d],
            recv_sem=out_recv_sem.at[d],
            device_id={"pages": d},
            device_id_type=MESH,
        ).wait_recv()
        pltpu.make_async_remote_copy(
            src_ref=stats_send.at[d],
            dst_ref=got_stats.at[d],
            send_sem=stats_send_sem.at[d],
            recv_sem=stats_recv_sem.at[d],
            device_id={"pages": d},
            device_id_type=MESH,
        ).wait_recv()
        return 0

    lax.fori_loop(1, n, finish, 0)

    def drain(row, _):
        src = row * 2 + y
        for i in range(reqs):
            q_copy(q_all.at[src, i], src, i, 2, partner).wait_send()

            @pl.when((row <= z) & (z + 1 < depth))
            def _():
                q_copy(q_all.at[src, i], src, i, 0, me + 2).wait_send()

            @pl.when((row >= z) & (z > 0))
            def _():
                q_copy(q_all.at[src, i], src, i, 1, me - 2).wait_send()

        return 0

    lax.fori_loop(0, depth, drain, 0)


def combine(cap, slots, target, used, tree_out, tree_stats, *refs):
    outs, stats, attended = refs[:slots], refs[slots : 2 * slots], refs[2 * slots]
    r = pl.program_id(0)
    tree_peak, tree_total = tree_stats[0, :, :QH], tree_stats[0, :, QH : 2 * QH]
    peaks, totals = [], []
    for j in range(slots):
        c = target[r * slots + j] % cap
        held = stats[j][0, :, : 2 * QH]
        for other in range(1, cap):
            held = jnp.where(
                c == other, stats[j][0, :, other * 2 * QH : (other + 1) * 2 * QH], held
            )
        peaks.append(jnp.where(used[r * slots + j] > 0, held[:, :QH], NEG_BIG))
        totals.append(held[:, QH:])
    top = tree_peak
    for peak in peaks:
        top = jnp.maximum(top, peak)
    tree_scale = jnp.exp(tree_peak - top)
    scales = [
        jnp.where(used[r * slots + j] > 0, jnp.exp(peaks[j] - top), 0.0) for j in range(slots)
    ]
    total = tree_total * tree_scale
    for j in range(slots):
        total = total + scales[j] * totals[j]
    for h in range(QH):
        mixed = tree_out[0, :, head(h)] * tree_scale[:, h : h + 1]
        for j in range(slots):
            mixed = mixed + outs[j][0, :, head(h)].astype(jnp.float32) * scales[j][:, h : h + 1]
        attended[0, :, head(h)] = (mixed / total[:, h : h + 1]).astype(jnp.bfloat16)


def shards(
    queries,
    tree_keys,
    tree_values,
    page_keys,
    page_values,
    page_table,
    prefix_lengths,
    tree_parents,
    live_lengths,
):
    n = lax.axis_size("pages")
    me = lax.axis_index("pages")
    reqs, tree, width = queries.shape
    pages_here, page_size, _ = page_keys.shape
    slots = page_table.shape[1]
    pairs = reqs * slots
    cap = max(1, pairs // n)

    mine = jnp.concatenate([page_table.reshape(-1), prefix_lengths, live_lengths])
    every = lax.all_gather(mine, "pages", axis=0, tiled=False)
    table = every[:, :pairs]
    prefix = jnp.repeat(every[:, pairs : pairs + reqs], slots, axis=1)
    lives = jnp.repeat(every[:, pairs + reqs :], slots, axis=1)
    pair = jnp.arange(pairs, dtype=jnp.int32)
    slot, req = pair % slots, pair // slots
    counts = jnp.clip(prefix - slot[None, :] * page_size, 0, page_size)
    local = table - me * pages_here
    here = (counts > 0) & (local >= 0) & (local < pages_here)
    before = pair[None, :] < pair[:, None]
    rank = jnp.sum((here[:, None, :] & before[None]).astype(jnp.int32), axis=2)
    take = here[:, None, :] & (rank[:, None, :] == jnp.arange(cap, dtype=jnp.int32)[None, :, None])
    facts = jnp.stack([local, counts, jnp.broadcast_to(req[None], local.shape)], axis=1)
    meta = jnp.sum(jnp.where(take[:, :, None, :], facts[:, None], 0), axis=3).reshape(-1)
    local_pages = jnp.arange(pages_here, dtype=jnp.int32)
    hit = here[None] & (local[None] == local_pages[:, None, None])
    reads = jnp.sum(jnp.where(hit, lives[None], 0), axis=(1, 2)).astype(jnp.int32)

    my_pages = page_table.reshape(-1)
    my_used = jnp.repeat(prefix_lengths, slots) > slot * page_size
    owners = my_pages // pages_here
    my_rank = jnp.sum(
        ((owners[:, None] == owners[None, :]) & my_used[None, :] & before).astype(jnp.int32),
        axis=1,
    )
    target = jnp.where(my_used, owners * cap + my_rank, me * cap)
    used = my_used.astype(jnp.int32)

    index = jnp.arange(tree, dtype=jnp.int32)
    links = (
        (index[None, None, :] == tree_parents[:, :, None])
        | (index[None, :, None] == index[None, None, :])
    ).astype(jnp.bfloat16)

    smem = pl.BlockSpec(memory_space=pltpu.SMEM)
    vmem = pl.BlockSpec(memory_space=pltpu.VMEM)
    hbm = pl.BlockSpec(memory_space=pl.ANY)
    depth = n // 2
    got_out, got_stats, tree_out, tree_stats = pl.pallas_call(
        functools.partial(exchange, n, cap),
        out_shape=(
            jax.ShapeDtypeStruct((n, cap, tree, width), jnp.bfloat16),
            jax.ShapeDtypeStruct((n, tree, HD), jnp.float32),
            jax.ShapeDtypeStruct((reqs, tree, width), jnp.float32),
            jax.ShapeDtypeStruct((reqs, tree, HD), jnp.float32),
        ),
        in_specs=[smem, smem] + [vmem] * 6,
        out_specs=(hbm, hbm, vmem, vmem),
        scratch_shapes=[
            pltpu.VMEM((n, reqs, tree, width), jnp.bfloat16),
            pltpu.VMEM((reqs, tree, width), jnp.bfloat16),
            pltpu.VMEM((n, cap, tree, width), jnp.bfloat16),
            pltpu.VMEM((n, tree, HD), jnp.float32),
            pltpu.SemaphoreType.DMA((3, depth, reqs)),
            pltpu.SemaphoreType.DMA((n, reqs)),
            pltpu.SemaphoreType.DMA((n,)),
            pltpu.SemaphoreType.DMA((n,)),
            pltpu.SemaphoreType.DMA((n,)),
            pltpu.SemaphoreType.DMA((n,)),
            pltpu.SemaphoreType.DMA((2,)),
        ],
        compiler_params=pltpu.CompilerParams(
            collective_id=0, has_side_effects=True, vmem_limit_bytes=62 * 1024 * 1024
        ),
        name="exchange",
    )(meta, live_lengths, queries, tree_keys, tree_values, links, page_keys, page_values)

    def own(r, *_):
        return (r, 0, 0)

    def out_at(j):
        return lambda r, target, used: (target[r * slots + j], 0, 0)

    def stats_at(j):
        return lambda r, target, used: (target[r * slots + j] // cap, 0, 0)

    got_out = got_out.reshape(n * cap, tree, width)
    attended = pl.pallas_call(
        functools.partial(combine, cap, slots),
        out_shape=jax.ShapeDtypeStruct((reqs, tree, width), jnp.bfloat16),
        grid_spec=pltpu.PrefetchScalarGridSpec(
            num_scalar_prefetch=2,
            grid=(reqs,),
            in_specs=[pl.BlockSpec((1, tree, width), own), pl.BlockSpec((1, tree, HD), own)]
            + [pl.BlockSpec((1, tree, width), out_at(j)) for j in range(slots)]
            + [pl.BlockSpec((1, tree, HD), stats_at(j)) for j in range(slots)],
            out_specs=pl.BlockSpec((1, tree, width), own),
        ),
        name="combine",
    )(target, used, tree_out, tree_stats, *([got_out] * slots), *([got_stats] * slots))
    return (attended, reads)


def solution(mesh):
    rows = P(("grp", "pages"), None, None)
    return jax.shard_map(
        shards,
        mesh=mesh,
        in_specs=(
            rows,
            rows,
            rows,
            rows,
            rows,
            P(("grp", "pages"), None),
            P(("grp", "pages")),
            P(("grp", "pages"), None),
            P(("grp", "pages")),
        ),
        out_specs=(rows, P(("grp", "pages"))),
        check_vma=False,
    )
```

time: 292 us -> 188 us (0.64)
  the two profiles are of different devices: /device:TPU:8 before, /device:TPU:0 now
where the time goes in v1:
time: 188 us
  Pallas kernels  164 us (87%)
  blocking collectives  13.1 us (7%)
  other arithmetic  4.81 us (3%)
  local copies, waits for them, and re-layouts  4.12 us (2%)
    pallas_call x1, Pallas kernels, shards(): pl.pallas_call(functools.partial(exchange, n, cap), out_shape=(jax.ShapeD...  156 us
    unnamed x1, blocking collectives  13.1 us
    pallas_call x1, Pallas kernels, shards(): pl.pallas_call(functools.partial(combine, cap, slots), out_shape=jax.Shap...  8.39 us

profile of v1, /device:TPU:0, one launch (start us, length us, event | category | flops | bytes accessed | tf_op | source)
XLA Modules:
  0.0 187.8 jit_solution(5972741851156636946)
XLA Ops:
  0.6 1.2 dynamic-slice
  2.5 0.8 reshape.162
  3.3 0.8 add_dynamic-update-slice_fusion
  4.2 13.1 %all-reduce = s32[192]{0:T(256)S(1)} all-reduce(s32[192]{0:T(256)S(1)} %add_dynamic-update-slice_fusion), channel_id=2, replica_groups=mesh['grp'=4,'pages'=8] {'pages'}, use_global_device_ids=true, to_apply=%add | all-reduce | flops 192 | bytes 1536
  17.3 0.7 broadcast_in_dim.44
  18.0 0.1 reshape.161
  18.1 0.6 fusion.8
  18.7 0.2 convert_reduce_fusion.1
  18.9 0.5 add_select_fusion.target
  19.4 0.1 reshape.167
  19.5 0.1 fusion.9
  19.6 0.1 copy.29
  19.7 0.1 copy.25
  19.7 0.1 copy.26
  19.8 0.2 convert_reduce_fusion
  20.1 0.1 copy.27
  20.2 0.2 select_reduce_fusion.1
  20.3 0.1 copy.28
  20.4 0.7 reshape.165.meta
  21.1 0.1 copy.30
  21.2 0.8 select_reduce_fusion
  21.9 1.4 fusion.1.link_ref
  23.4 156.0 %exchange.1 = (bf16[8,2,64,2048]{3,2,1,0:T(8,128)(2,1)}, f32[8,64,128]{2,1,0:T(8,128)}, f32[4,64,2048]{2,1,0:T(8,128)}, f32[4,64,128]{2,1,0:T(8,128)}) custom-call(s32[48]{0:T(128)} %reshape.165.meta, s32[4]{0:T(128)} %live.1, bf16[4,64,2048]{2,1,0:T(8,128)(2,1)} %q_ref.1, bf16[4,64,512]{2,1,0:T(8,128)(2,1)} %tk_ref.1, bf16[4,64,512]{2,1,0:T(8,128)(2,1)} %tv_ref.1, ...), custom_call_target="tpu_custom_call" | custom-call | tf_op jit(solution)/shard_map/exchange/pallas_call | solution.py:386
  179.4 8.4 %combine.1 = bf16[4,64,2048]{2,1,0:T(8,128)(2,1)} custom-call(s32[16]{0:T(128)} %add_select_fusion.target, s32[16]{0:T(128)} %get-tuple-element.14.used, f32[4,64,2048]{2,1,0:T(8,128)} %get-tuple-element.6.tree_out, f32[4,64,128]{2,1,0:T(8,128)} %get-tuple-element.7.tree_stats, bf16[16,64,2048]{2,1,0:T(8,128)(2,1)} %bitcast.6, ...), custom_call_target="tpu_custom_call" | custom-call | tf_op jit(solution)/shard_map/combine/pallas_call | solution.py:425
  (13 shorter events, 0.1 us)

commit v2 on v1

--- a/solution.py
+++ b/solution.py
@@ -47,14 +47,22 @@
 def exchange(
     n,
     cap,
-    meta,
     live,
+    target,
+    used,
+    label_ref,
     q_ref,
     tk_ref,
     tv_ref,
     link_ref,
+    pk_hbm,
+    pv_hbm,
+    attended,
+    reads_ref,
     pk_ref,
     pv_ref,
+    labels,
+    label_now,
     got_out,
     got_stats,
     tree_out,
@@ -63,6 +71,8 @@
     q_now,
     out_send,
     stats_send,
+    label_send_sem,
+    label_recv_sem,
     q_send_sem,
     q_recv_sem,
     out_send_sem,
@@ -72,12 +82,21 @@
     local_sem,
 ):
     reqs, tree, _ = q_ref.shape
-    page = pk_ref.shape[1]
+    pages_here, page, _ = pk_ref.shape
+    slots = target.shape[0] // reqs
+    lanes = cap * 2 * QH
+    fold = HD // lanes
+    rows_held = tree // fold
     depth = n // 2
     me = lax.axis_index("pages")
     z, y = me // 2, me % 2
     other = 1 - y
     partner = z * 2 + other
+
+    load_keys = pltpu.make_async_copy(pk_hbm, pk_ref, local_sem.at[2])
+    load_values = pltpu.make_async_copy(pv_hbm, pv_ref, local_sem.at[3])
+    load_keys.start()
+    load_values.start()
 
     barrier = pltpu.get_barrier_semaphore()
 
@@ -103,7 +122,7 @@
     def out_copy(d):
         return pltpu.make_async_remote_copy(
             src_ref=out_send.at[d],
-            dst_ref=got_out.at[me],
+            dst_ref=got_out.at[pl.ds(me * cap, cap)],
             send_sem=out_send_sem.at[d],
             recv_sem=out_recv_sem.at[me],
             device_id={"pages": d},
@@ -130,6 +149,22 @@
             device_id_type=MESH,
         ).wait_recv()
 
+    def label_copy(d):
+        return pltpu.make_async_remote_copy(
+            src_ref=label_ref.at[d],
+            dst_ref=labels.at[me],
+            send_sem=label_send_sem.at[d],
+            recv_sem=label_recv_sem.at[me],
+            device_id={"pages": d},
+            device_id_type=MESH,
+        )
+
+    def tell(i, _):
+        label_copy((me + i) % n).start()
+        return 0
+
+    lax.fori_loop(1, n, tell, 0)
+
     for i in range(reqs):
         q_copy(q_ref.at[i], me, i, 2, partner).start()
 
@@ -147,8 +182,7 @@
     def serve(d):
         stats = jnp.zeros((tree, HD), jnp.float32)
         for c in range(cap):
-            base = (d * cap + c) * 3
-            which, count, req = meta[base], meta[base + 1], meta[base + 2]
+            which, count, req = (label_now[d, 0, c * 4 + f] for f in range(3))
 
             def out_to(h, value):
                 out_send[d, c, :, head(h)] = value.astype(jnp.bfloat16)
@@ -163,14 +197,9 @@
                 lane,
                 c * 2 * QH,
             )
-        stats_send[d] = stats
-
-    q_now[...] = q_ref[...]
-    serve(me)
-    own_out = pltpu.make_async_copy(out_send.at[me], got_out.at[me], local_sem.at[0])
-    own_stats = pltpu.make_async_copy(stats_send.at[me], got_stats.at[me], local_sem.at[1])
-    own_out.start()
-    own_stats.start()
+        stats_send[d] = jnp.concatenate(
+            [stats[i * rows_held : (i + 1) * rows_held, :lanes] for i in range(fold)], axis=1
+        )
 
     def one_tree(r, _):
         reach = link_ref[r]
@@ -199,6 +228,46 @@
 
     lax.fori_loop(0, reqs, one_tree, 0)
 
+    labels[me] = label_ref[me]
+
+    def hear(i, _):
+        d = (me + i) % n
+        pltpu.make_async_remote_copy(
+            src_ref=label_ref.at[d],
+            dst_ref=labels.at[d],
+            send_sem=label_send_sem.at[d],
+            recv_sem=label_recv_sem.at[d],
+            device_id={"pages": d},
+            device_id_type=MESH,
+        ).wait()
+        return 0
+
+    lax.fori_loop(1, n, hear, 0)
+    into_scalars = pltpu.make_async_copy(labels, label_now, local_sem.at[0])
+    into_scalars.start()
+    into_scalars.wait()
+    load_keys.wait()
+    load_values.wait()
+
+    q_now[...] = q_ref[...]
+    serve(me)
+    for c in range(cap):
+        got_out[me * cap + c] = out_send[me, c]
+    got_stats[me] = stats_send[me]
+
+    page_row = lax.broadcasted_iota(jnp.int32, (pages_here, HD), 0)
+
+    def count_reads(d, reads):
+        for c in range(cap):
+            which, count, _, lives = (label_now[d, 0, c * 4 + f] for f in range(4))
+            lives = jnp.where(count > 0, lives, 0)
+            reads = reads + jnp.where(page_row == which, lives, 0)
+        return reads
+
+    reads_ref[...] = lax.fori_loop(
+        0, n, count_reads, jnp.zeros((pages_here, HD), jnp.int32)
+    )
+
     def step(s, _):
         for i in range(reqs):
 
@@ -249,16 +318,13 @@
 
     lax.fori_loop(1, depth + 1, step, 0)
 
-    own_out.wait()
-    own_stats.wait()
-
     def finish(i, _):
         d = (me + i) % n
         out_copy(d).wait_send()
         stats_copy(d).wait_send()
         pltpu.make_async_remote_copy(
             src_ref=out_send.at[d],
-            dst_ref=got_out.at[d],
+            dst_ref=got_out.at[pl.ds(d * cap, cap)],
             send_sem=out_send_sem.at[d],
             recv_sem=out_recv_sem.at[d],
             device_id={"pages": d},
@@ -293,36 +359,44 @@
 
     lax.fori_loop(0, depth, drain, 0)
 
-
-def combine(cap, slots, target, used, tree_out, tree_stats, *refs):
-    outs, stats, attended = refs[:slots], refs[slots : 2 * slots], refs[2 * slots]
-    r = pl.program_id(0)
-    tree_peak, tree_total = tree_stats[0, :, :QH], tree_stats[0, :, QH : 2 * QH]
-    peaks, totals = [], []
-    for j in range(slots):
-        c = target[r * slots + j] % cap
-        held = stats[j][0, :, : 2 * QH]
-        for other in range(1, cap):
-            held = jnp.where(
-                c == other, stats[j][0, :, other * 2 * QH : (other + 1) * 2 * QH], held
+    def merge(r, _):
+        tree_peak, tree_total = tree_stats[r, :, :QH], tree_stats[r, :, QH : 2 * QH]
+        top = tree_peak
+        peaks, totals = [], []
+        for j in range(slots):
+            where_ = target[r * slots + j]
+            live_slot = used[r * slots + j] > 0
+            packed = got_stats[where_ // cap]
+            held = jnp.concatenate(
+                [packed[:, i * lanes : (i + 1) * lanes] for i in range(fold)], axis=0
             )
-        peaks.append(jnp.where(used[r * slots + j] > 0, held[:, :QH], NEG_BIG))
-        totals.append(held[:, QH:])
-    top = tree_peak
-    for peak in peaks:
-        top = jnp.maximum(top, peak)
-    tree_scale = jnp.exp(tree_peak - top)
-    scales = [
-        jnp.where(used[r * slots + j] > 0, jnp.exp(peaks[j] - top), 0.0) for j in range(slots)
-    ]
-    total = tree_total * tree_scale
-    for j in range(slots):
-        total = total + scales[j] * totals[j]
-    for h in range(QH):
-        mixed = tree_out[0, :, head(h)] * tree_scale[:, h : h + 1]
+            mine = held[:, : 2 * QH]
+            for c in range(1, cap):
+                mine = jnp.where(
+                    where_ % cap == c, held[:, c * 2 * QH : (c + 1) * 2 * QH], mine
+                )
+            peaks.append(jnp.where(live_slot, mine[:, :QH], NEG_BIG))
+            totals.append(mine[:, QH:])
+            top = jnp.maximum(top, peaks[j])
+        tree_scale = jnp.exp(tree_peak - top)
+        scales = [
+            jnp.where(used[r * slots + j] > 0, jnp.exp(peaks[j] - top), 0.0)
+            for j in range(slots)
+        ]
+        total = tree_total * tree_scale
         for j in range(slots):
-            mixed = mixed + outs[j][0, :, head(h)].astype(jnp.float32) * scales[j][:, h : h + 1]
-        attended[0, :, head(h)] = (mixed / total[:, h : h + 1]).astype(jnp.bfloat16)
+            total = total + scales[j] * totals[j]
+        tree_scale = tree_scale / total
+        scales = [scale / total for scale in scales]
+        for h in range(QH):
+            mixed = tree_out[r, :, head(h)] * tree_scale[:, h : h + 1]
+            for j in range(slots):
+                part = got_out[target[r * slots + j], :, head(h)].astype(jnp.float32)
+                mixed = mixed + part * scales[j][:, h : h + 1]
+            attended[r, :, head(h)] = mixed.astype(jnp.bfloat16)
+        return 0
+
+    lax.fori_loop(0, reqs, merge, 0)
 
 
 def shards(
@@ -344,34 +418,27 @@
     pairs = reqs * slots
     cap = max(1, pairs // n)
 
-    mine = jnp.concatenate([page_table.reshape(-1), prefix_lengths, live_lengths])
-    every = lax.all_gather(mine, "pages", axis=0, tiled=False)
-    table = every[:, :pairs]
-    prefix = jnp.repeat(every[:, pairs : pairs + reqs], slots, axis=1)
-    lives = jnp.repeat(every[:, pairs + reqs :], slots, axis=1)
     pair = jnp.arange(pairs, dtype=jnp.int32)
-    slot, req = pair % slots, pair // slots
-    counts = jnp.clip(prefix - slot[None, :] * page_size, 0, page_size)
-    local = table - me * pages_here
-    here = (counts > 0) & (local >= 0) & (local < pages_here)
+    my_pages = page_table.reshape(-1)
+    my_counts = jnp.clip(
+        jnp.repeat(prefix_lengths, slots) - pair % slots * page_size, 0, page_size
+    )
+    my_used = my_counts > 0
+    owners = my_pages // pages_here
     before = pair[None, :] < pair[:, None]
-    rank = jnp.sum((here[:, None, :] & before[None]).astype(jnp.int32), axis=2)
-    take = here[:, None, :] & (rank[:, None, :] == jnp.arange(cap, dtype=jnp.int32)[None, :, None])
-    facts = jnp.stack([local, counts, jnp.broadcast_to(req[None], local.shape)], axis=1)
-    meta = jnp.sum(jnp.where(take[:, :, None, :], facts[:, None], 0), axis=3).reshape(-1)
-    local_pages = jnp.arange(pages_here, dtype=jnp.int32)
-    hit = here[None] & (local[None] == local_pages[:, None, None])
-    reads = jnp.sum(jnp.where(hit, lives[None], 0), axis=(1, 2)).astype(jnp.int32)
-
-    my_pages = page_table.reshape(-1)
-    my_used = jnp.repeat(prefix_lengths, slots) > slot * page_size
-    owners = my_pages // pages_here
-    my_rank = jnp.sum(
+    rank = jnp.sum(
         ((owners[:, None] == owners[None, :]) & my_used[None, :] & before).astype(jnp.int32),
         axis=1,
     )
-    target = jnp.where(my_used, owners * cap + my_rank, me * cap)
+    target = jnp.where(my_used, owners * cap + rank, me * cap)
     used = my_used.astype(jnp.int32)
+    facts = jnp.stack(
+        [my_pages % pages_here, my_counts, pair // slots, jnp.repeat(live_lengths, slots)]
+    )
+    place = jnp.arange(n * cap, dtype=jnp.int32)
+    take = my_used[None, :] & (target[None, :] == place[:, None])
+    labels = jnp.sum(jnp.where(take[:, None, :], facts[None], 0), axis=2)
+    labels = jnp.pad(labels.reshape(n, 1, cap * 4), ((0, 0), (0, 7), (0, HD - cap * 4)))
 
     index = jnp.arange(tree, dtype=jnp.int32)
     links = (
@@ -383,59 +450,55 @@
     vmem = pl.BlockSpec(memory_space=pltpu.VMEM)
     hbm = pl.BlockSpec(memory_space=pl.ANY)
     depth = n // 2
-    got_out, got_stats, tree_out, tree_stats = pl.pallas_call(
+    held_stats = (n, tree * cap * 2 * QH // HD, HD)
+    attended, reads = pl.pallas_call(
         functools.partial(exchange, n, cap),
         out_shape=(
-            jax.ShapeDtypeStruct((n, cap, tree, width), jnp.bfloat16),
-            jax.ShapeDtypeStruct((n, tree, HD), jnp.float32),
-            jax.ShapeDtypeStruct((reqs, tree, width), jnp.float32),
-            jax.ShapeDtypeStruct((reqs, tree, HD), jnp.float32),
+            jax.ShapeDtypeStruct((reqs, tree, width), jnp.bfloat16),
+            jax.ShapeDtypeStruct((pages_here, HD), jnp.int32),
         ),
-        in_specs=[smem, smem] + [vmem] * 6,
-        out_specs=(hbm, hbm, vmem, vmem),
+        in_specs=[smem] * 3 + [vmem] * 5 + [hbm] * 2,
+        out_specs=(vmem, vmem),
         scratch_shapes=[
+            pltpu.VMEM(page_keys.shape, jnp.bfloat16),
+            pltpu.VMEM(page_values.shape, jnp.bfloat16),
+            pltpu.VMEM((n, 8, HD), jnp.int32),
+            pltpu.SMEM((n, 8, HD), jnp.int32),
+            pltpu.VMEM((n * cap, tree, width), jnp.bfloat16),
+            pltpu.VMEM(held_stats, jnp.float32),
+            pltpu.VMEM((reqs, tree, width), jnp.float32),
+            pltpu.VMEM((reqs, tree, HD), jnp.float32),
             pltpu.VMEM((n, reqs, tree, width), jnp.bfloat16),
             pltpu.VMEM((reqs, tree, width), jnp.bfloat16),
             pltpu.VMEM((n, cap, tree, width), jnp.bfloat16),
-            pltpu.VMEM((n, tree, HD), jnp.float32),
+            pltpu.VMEM(held_stats, jnp.float32),
+            pltpu.SemaphoreType.DMA((n,)),
+            pltpu.SemaphoreType.DMA((n,)),
             pltpu.SemaphoreType.DMA((3, depth, reqs)),
             pltpu.SemaphoreType.DMA((n, reqs)),
             pltpu.SemaphoreType.DMA((n,)),
             pltpu.SemaphoreType.DMA((n,)),
             pltpu.SemaphoreType.DMA((n,)),
             pltpu.SemaphoreType.DMA((n,)),
-            pltpu.SemaphoreType.DMA((2,)),
+            pltpu.SemaphoreType.DMA((4,)),
         ],
         compiler_params=pltpu.CompilerParams(
-            collective_id=0, has_side_effects=True, vmem_limit_bytes=62 * 1024 * 1024
+            collective_id=0, has_side_effects=True, vmem_limit_bytes=63 * 1024 * 1024
         ),
         name="exchange",
-    )(meta, live_lengths, queries, tree_keys, tree_values, links, page_keys, page_values)
-
-    def own(r, *_):
-        return (r, 0, 0)
-
-    def out_at(j):
-        return lambda r, target, used: (target[r * slots + j], 0, 0)
-
-    def stats_at(j):
-        return lambda r, target, used: (target[r * slots + j] // cap, 0, 0)
-
-    got_out = got_out.reshape(n * cap, tree, width)
-    attended = pl.pallas_call(
-        functools.partial(combine, cap, slots),
-        out_shape=jax.ShapeDtypeStruct((reqs, tree, width), jnp.bfloat16),
-        grid_spec=pltpu.PrefetchScalarGridSpec(
-            num_scalar_prefetch=2,
-            grid=(reqs,),
-            in_specs=[pl.BlockSpec((1, tree, width), own), pl.BlockSpec((1, tree, HD), own)]
-            + [pl.BlockSpec((1, tree, width), out_at(j)) for j in range(slots)]
-            + [pl.BlockSpec((1, tree, HD), stats_at(j)) for j in range(slots)],
-            out_specs=pl.BlockSpec((1, tree, width), own),
-        ),
-        name="combine",
-    )(target, used, tree_out, tree_stats, *([got_out] * slots), *([got_stats] * slots))
-    return (attended, reads)
+    )(
+        live_lengths,
+        target,
+        used,
+        labels,
+        queries,
+        tree_keys,
+        tree_values,
+        links,
+        page_keys,
+        page_values,
+    )
+    return (attended, reads[:, 0])
 
 
 def solution(mesh):

time: 188 us -> 177 us (0.941)
  blocking collectives: 13.1 us -> 0 us
  local copies, waits for them, and re-layouts: 4.12 us -> 7.6 us
  other arithmetic: 4.81 us -> 2.34 us
  Pallas kernels: 164 us -> 166 us
    unnamed x1 -> x0, blocking collectives: 13.1 us -> none
    pallas_call x1, Pallas kernels: 156 us -> 166 us  [shards(): pl.pallas_call(functools.partial(exchange, n, cap), out_shape=(jax.ShapeD...]
    pallas_call x1 -> x0, Pallas kernels: 8.39 us -> none  [shards(): pl.pallas_call(functools.partial(combine, cap, slots), out_shape=jax.Shap...]
where the time goes in v2:
time: 177 us
  Pallas kernels  166 us (94%)
  local copies, waits for them, and re-layouts  7.6 us (4%)
  other arithmetic  2.34 us (1%)
    pallas_call x1, Pallas kernels, shards(): pl.pallas_call(functools.partial(exchange, n, cap), out_shape=(jax.ShapeD...  166 us

profile of v2, /device:TPU:0, one launch (start us, length us, event | category | flops | bytes accessed | tf_op | source)
XLA Modules:
  0.0 177.1 jit_solution(3058864544669142622)
XLA Ops:
  0.6 0.8 reshape.259
  1.4 0.8 reshape.260
  2.2 0.7 broadcast_in_dim.28
  2.9 0.1 reshape.261
  3.0 0.1 reshape.258
  3.1 0.5 fusion.10
  3.6 0.2 convert_reduce_fusion
  3.8 0.0 copy-start
  3.8 0.7 broadcast_in_dim.31
  4.6 0.1 stack_reshape.3
  4.7 0.1 select_reduce_fusion
  4.8 0.1 copy.13
  4.9 0.1 reshape.262
  5.0 0.6 pad.4.label_ref
  5.6 1.4 fusion.1.link_ref
  7.0 0.0 copy-done
  7.0 166.5 %exchange.1 = (bf16[4,64,2048]{2,1,0:T(8,128)(2,1)}, s32[8,128]{1,0:T(8,128)}) custom-call(s32[4]{0:T(128)} %live.1, s32[16]{0:T(128)} %copy-done, s32[16]{0:T(128)} %get-tuple-element.6.used, s32[8,8,128]{2,1,0:T(8,128)} %pad.4.label_ref, bf16[4,64,2048]{2,1,0:T(8,128)(2,1)} %q_ref.1, bf16[4,64,512]{2,1,0:T(8,128)(2,1)} %tk_ref.1, ...), custom_call_target="tpu_custom_call" | custom-call | tf_op jit(solution)/shard_map/exchange/pallas_call | solution.py:454
  173.5 1.3 slice_reduce_fusion
  174.8 2.3 %copy.16 = bf16[4,64,2048]{2,1,0:T(8,128)(2,1)} copy(bf16[4,64,2048]{2,1,0:T(8,128)(2,1)} %get-tuple-element.12) | data formatting | bytes 2097152
  (7 shorter events, 0.1 us)
Async XLA Ops:
  3.8 3.2 %copy-start = (s32[16]{0:T(128)}, s32[16]{0:T(128)S(1)}, u32[]{:S(2)}) copy-start(s32[16]{0:T(128)S(1)} %add_select_fusion.target) | copy-start | bytes 196

commit v3 on v2

--- a/solution.py
+++ b/solution.py
@@ -47,20 +47,22 @@
 def exchange(
     n,
     cap,
+    table,
+    prefix,
     live,
-    target,
-    used,
-    label_ref,
+    parents_ref,
     q_ref,
     tk_ref,
     tv_ref,
-    link_ref,
     pk_hbm,
     pv_hbm,
     attended,
     reads_ref,
     pk_ref,
     pv_ref,
+    target,
+    used,
+    label_ref,
     labels,
     label_now,
     got_out,
@@ -83,7 +85,7 @@
 ):
     reqs, tree, _ = q_ref.shape
     pages_here, page, _ = pk_ref.shape
-    slots = target.shape[0] // reqs
+    slots = table.shape[1]
     lanes = cap * 2 * QH
     fold = HD // lanes
     rows_held = tree // fold
@@ -149,6 +151,41 @@
             device_id_type=MESH,
         ).wait_recv()
 
+    for i in range(reqs):
+        q_copy(q_ref.at[i], me, i, 2, partner).start()
+
+        @pl.when(z + 1 < depth)
+        def _():
+            q_copy(q_ref.at[i], me, i, 0, me + 2).start()
+
+        @pl.when(z > 0)
+        def _():
+            q_copy(q_ref.at[i], me, i, 1, me - 2).start()
+
+    label_row = lax.broadcasted_iota(jnp.int32, (n, HD), 0)
+    label_lane = lax.broadcasted_iota(jnp.int32, (n, HD), 1)
+    told = jnp.zeros((n, HD), jnp.int32)
+    owners, taken = [], []
+    for p in range(reqs * slots):
+        r, j = p // slots, p % slots
+        count = jnp.clip(prefix[r] - j * page, 0, page)
+        owner = lax.div(table[r, j], jnp.int32(pages_here))
+        rank = jnp.int32(0)
+        for earlier in range(p):
+            same = (owners[earlier] == owner) & (taken[earlier] > 0)
+            rank = rank + jnp.where(same, 1, 0)
+        takes = jnp.where(count > 0, 1, 0)
+        owners.append(owner)
+        taken.append(takes)
+        used[p] = takes
+        target[p] = jnp.where(count > 0, owner * cap + rank, me * cap)
+        row = label_row == jnp.where(count > 0, owner, -1)
+        facts = (table[r, j] - owner * pages_here, count, r, live[r])
+        for f, fact in enumerate(facts):
+            told = jnp.where(row & (label_lane == rank * 4 + f), fact, told)
+    for d in range(n):
+        label_ref[d, 0:1, :] = told[d : d + 1]
+
     def label_copy(d):
         return pltpu.make_async_remote_copy(
             src_ref=label_ref.at[d],
@@ -164,17 +201,6 @@
         return 0
 
     lax.fori_loop(1, n, tell, 0)
-
-    for i in range(reqs):
-        q_copy(q_ref.at[i], me, i, 2, partner).start()
-
-        @pl.when(z + 1 < depth)
-        def _():
-            q_copy(q_ref.at[i], me, i, 0, me + 2).start()
-
-        @pl.when(z > 0)
-        def _():
-            q_copy(q_ref.at[i], me, i, 1, me - 2).start()
 
     lane = lax.broadcasted_iota(jnp.int32, (tree, HD), 1)
     key_lane = lax.broadcasted_iota(jnp.int32, (GROUPS * tree, page), 1)
@@ -202,13 +228,19 @@
         )
 
     def one_tree(r, _):
-        reach = link_ref[r]
+        source = lax.broadcasted_iota(jnp.int32, (tree, tree), 0)
+        child = lax.broadcasted_iota(jnp.int32, (tree, tree), 1)
+        linked = (source == parents_ref[pl.ds(r, 1), :]) | (source == child)
+        same = jnp.where(source == child, 1.0, 0.0).astype(jnp.bfloat16)
+        reach = jnp.where(linked, 1.0, 0.0).astype(jnp.bfloat16)
         for level in range((tree - 1).bit_length()):
             reach = jnp.where(
                 jnp.dot(reach, reach, preferred_element_type=jnp.float32) > 0, 1.0, 0.0
             ).astype(jnp.bfloat16)
-        seen = lax.broadcasted_iota(jnp.int32, (tree, tree), 1) < live[r]
-        open_ = jnp.where(seen, reach.astype(jnp.float32), 0.0)
+        upright = lax.dot_general(
+            reach, same, (((0,), (0,)), ((), ())), preferred_element_type=jnp.float32
+        )
+        open_ = jnp.where(child < live[r], upright, 0.0)
         allowed = jnp.concatenate([open_] * GROUPS, axis=0) > 0
 
         def out_to(h, value):
@@ -411,40 +443,11 @@
     live_lengths,
 ):
     n = lax.axis_size("pages")
-    me = lax.axis_index("pages")
     reqs, tree, width = queries.shape
-    pages_here, page_size, _ = page_keys.shape
+    pages_here = page_keys.shape[0]
     slots = page_table.shape[1]
     pairs = reqs * slots
     cap = max(1, pairs // n)
-
-    pair = jnp.arange(pairs, dtype=jnp.int32)
-    my_pages = page_table.reshape(-1)
-    my_counts = jnp.clip(
-        jnp.repeat(prefix_lengths, slots) - pair % slots * page_size, 0, page_size
-    )
-    my_used = my_counts > 0
-    owners = my_pages // pages_here
-    before = pair[None, :] < pair[:, None]
-    rank = jnp.sum(
-        ((owners[:, None] == owners[None, :]) & my_used[None, :] & before).astype(jnp.int32),
-        axis=1,
-    )
-    target = jnp.where(my_used, owners * cap + rank, me * cap)
-    used = my_used.astype(jnp.int32)
-    facts = jnp.stack(
-        [my_pages % pages_here, my_counts, pair // slots, jnp.repeat(live_lengths, slots)]
-    )
-    place = jnp.arange(n * cap, dtype=jnp.int32)
-    take = my_used[None, :] & (target[None, :] == place[:, None])
-    labels = jnp.sum(jnp.where(take[:, None, :], facts[None], 0), axis=2)
-    labels = jnp.pad(labels.reshape(n, 1, cap * 4), ((0, 0), (0, 7), (0, HD - cap * 4)))
-
-    index = jnp.arange(tree, dtype=jnp.int32)
-    links = (
-        (index[None, None, :] == tree_parents[:, :, None])
-        | (index[None, :, None] == index[None, None, :])
-    ).astype(jnp.bfloat16)
 
     smem = pl.BlockSpec(memory_space=pltpu.SMEM)
     vmem = pl.BlockSpec(memory_space=pltpu.VMEM)
@@ -457,11 +460,14 @@
             jax.ShapeDtypeStruct((reqs, tree, width), jnp.bfloat16),
             jax.ShapeDtypeStruct((pages_here, HD), jnp.int32),
         ),
-        in_specs=[smem] * 3 + [vmem] * 5 + [hbm] * 2,
+        in_specs=[smem] * 3 + [vmem] * 4 + [hbm] * 2,
         out_specs=(vmem, vmem),
         scratch_shapes=[
             pltpu.VMEM(page_keys.shape, jnp.bfloat16),
             pltpu.VMEM(page_values.shape, jnp.bfloat16),
+            pltpu.SMEM((pairs,), jnp.int32),
+            pltpu.SMEM((pairs,), jnp.int32),
+            pltpu.VMEM((n, 8, HD), jnp.int32),
             pltpu.VMEM((n, 8, HD), jnp.int32),
             pltpu.SMEM((n, 8, HD), jnp.int32),
             pltpu.VMEM((n * cap, tree, width), jnp.bfloat16),
@@ -487,14 +493,13 @@
         ),
         name="exchange",
     )(
+        page_table,
+        prefix_lengths,
         live_lengths,
-        target,
-        used,
-        labels,
+        tree_parents,
         queries,
         tree_keys,
         tree_values,
-        links,
         page_keys,
         page_values,
     )

time: 177 us -> 174 us (0.983)
  Pallas kernels: 166 us -> 170 us
  local copies, waits for them, and re-layouts: 7.6 us -> 3.6 us
  other arithmetic: 2.34 us -> 0 us
    pallas_call x1, Pallas kernels: 166 us -> 170 us  [shards(): pl.pallas_call(functools.partial(exchange, n, cap), out_shape=(jax.ShapeD...]
    convert_element_type x2 -> x0, other arithmetic: 1.93 us -> none  [the longest x1 1.41 us: shards(): links = ((index[None, None, :] == tree_parents[:, :, None]) | (index[None...]
where the time goes in v3:
time: 174 us
  Pallas kernels  170 us (98%)
  local copies, waits for them, and re-layouts  3.6 us (2%)
    pallas_call x1, Pallas kernels, shards(): pl.pallas_call(functools.partial(exchange, n, cap), out_shape=(jax.ShapeD...  170 us

profile of v3, /device:TPU:0, one launch (start us, length us, event | category | flops | bytes accessed | tf_op | source)
XLA Modules:
  0.0 173.9 jit_solution(9322006604113363124)
XLA Ops:
  0.6 169.7 %exchange.1 = (bf16[4,64,2048]{2,1,0:T(8,128)(2,1)}, s32[8,128]{1,0:T(8,128)}) custom-call(s32[4,4]{1,0:T(4,128)} %table.1, s32[4]{0:T(128)} %prefix.1, s32[4]{0:T(128)} %live.1, s32[4,64]{1,0:T(4,128)} %parents_ref.1, bf16[4,64,2048]{2,1,0:T(8,128)(2,1)} %q_ref.1, bf16[4,64,512]{2,1,0:T(8,128)(2,1)} %tk_ref.1, bf16[4,64,512]{2,1,0:T(8,128)(2,1)} %tv_ref.1, ...), custom_call_target="tpu_custom_call" | custom-call | tf_op jit(solution)/shard_map/exchange/pallas_call | solution.py:457
  170.3 1.3 slice_reduce_fusion
  171.6 2.3 %copy.12 = bf16[4,64,2048]{2,1,0:T(8,128)(2,1)} copy(bf16[4,64,2048]{2,1,0:T(8,128)(2,1)} %get-tuple-element.8) | data formatting | bytes 2097152
